TPU v7x, 32 devices: a whole 2x2x4 slice. The times are simulated.
32 devices in a mesh: slab: 8 (over y, x, core), det: 4 (over z).
Axes of the slice: x: 2, y: 2, z: 4, core: 2. Of those that a mesh axis runs over, the one named last changes fastest.
Arguments:
- traces: float32 [32, 128, 4096], P(('slab', 'det')), may hold values from -6 to 6
- tables: bfloat16 [32, 256, 2048], P('slab', None, 'det'), may hold values from -0.0625 to 0.0625
- slab_range: int32 [32, 2], P(('slab', 'det')), may hold values from 0 to 7, as said below
- table_slot: int32 [32, 7], P(('slab', 'det')), may hold values from 0 to 3
- sample_start: int32 [32, 7], P(('slab', 'det')), may hold values from 0 to 3840
Outputs:
- image: float32 [128, 16384], P(None, ('slab', 'det'))
Inputs may be any that keep to these rules, and one draw needn't show every extreme that they name: For detector d with home slab g = d // 4: max(0, g - 3) <= slab_range[d, 0] <= g <= slab_range[d, 1] <= min(7, g + 3); some detectors reach the full 3 on both sides where the grid allows.
All inputs are finite; a program needn't handle non-finite values.
Results may differ from a plain program's by a relative error of at most 0.007.
Values may be sent and summed in bfloat16 or wider, within the bound.
No kernel may reach another device: no remote copies, remote signals or barrier semaphores. Data moves between devices by JAX's collectives and lax.ppermute only.
A program may use at most 64 MiB of HBM per device.

v0:
```python
import jax
import jax.numpy as jnp
from jax import lax
from jax.sharding import PartitionSpec as P

KWIN = 256
NTAB = 4
RANGE = 3


def shifted(x, axis, by):
    peers = lax.axis_size(axis)
    pairs = [(i, i + by) for i in range(peers) if 0 <= i + by < peers]
    return lax.ppermute(x, axis, pairs)


def cut_windows(trace_rows, starts):

    def single(trace_row, first_index):
        return lax.dynamic_slice_in_dim(trace_row, first_index, KWIN, 1)

    return jax.vmap(single)(trace_rows, starts)


def bin_windows(windows, slot_ids, active):
    onehot = (slot_ids[:, None] == jnp.arange(NTAB, dtype=jnp.int32)[None, :]) & active[:, None]
    onehot = onehot.astype(jnp.bfloat16)
    return jnp.einsum("it,ifk->tfk", onehot, windows, preferred_element_type=jnp.float32)


def body(traces, tables, slab_range, table_slot, sample_start):
    position = lax.axis_index("slab")
    samples = traces.astype(jnp.bfloat16)
    own_active = (slab_range[:, 0] <= position) & (position <= slab_range[:, 1])
    stacked = bin_windows(
        cut_windows(samples, sample_start[:, RANGE]), table_slot[:, RANGE], own_active
    )
    for offset in list(range(-RANGE, 0)) + list(range(1, RANGE + 1)):
        target = position + offset
        active = (slab_range[:, 0] <= target) & (target <= slab_range[:, 1])
        windows = cut_windows(samples, sample_start[:, offset + RANGE])
        windows = windows * active[:, None, None].astype(jnp.bfloat16)
        arrived_windows, arrived_slots = shifted(
            (windows, table_slot[:, offset + RANGE]), "slab", offset
        )
        everything = jnp.ones(arrived_slots.shape, jnp.bool_)
        stacked = stacked + bin_windows(arrived_windows, arrived_slots, everything)
    binned = stacked.astype(jnp.bfloat16)
    partial_image = jnp.einsum(
        "tfk,tkv->fv",
        binned,
        lax.all_gather(tables, "det", axis=2, tiled=True),
        preferred_element_type=jnp.float32,
    )
    return lax.psum_scatter(partial_image, "det", scatter_dimension=1, tiled=True)


def solution(mesh):
    placed = (
        P(("slab", "det"), None, None),
        P("slab", None, "det"),
        P(("slab", "det"), None),
        P(("slab", "det"), None),
        P(("slab", "det"), None),
    )
    return jax.shard_map(
        body, mesh=mesh, in_specs=placed, out_specs=P(None, ("slab", "det")), check_vma=False
    )
```

profile of v0, /device:TPU:0, one launch (start us, length us, event | category | flops | bytes accessed | tf_op | source)
XLA Modules:
  0.0 129.3 jit_solution(1520195266104620349)
XLA Ops:
  6.5 0.7 all-gather.2.cloned.1.call-update
  7.3 0.0 reduce-scatter.2.cloned.1.call-start
  7.3 1.6 %fusion.21 = (s32[1,1]{1,0:T(1,128)}, s32[1,1]{1,0:T(1,128)}, s32[1,1]{1,0:T(1,128)}, s32[1,1]{1,0:T(1,128)}, s32[1,1]{1,0:T(1,128)}, /*index=5*/s32[1,1]{1,0:T(1,128)}, s32[1,1]{1,0:T(1,128)}) fusion(s32[1,7]{1,0:T(1,128)} %param.8), kind=kLoop, calls=%fused_computation.43 | loop fusion | bytes 56 | tf_op jit(solution)/shard_map/slice | solution.py:36
  8.9 3.0 %collective-permute-start.6 = (s32[1]{0:T(128)}, s32[1]{0:T(128)}, u32[]{:S(2)}, u32[]{:S(2)}) collective-permute-start(s32[1]{0:T(128)} %bitcast.33), channel_id=1, source_target_pairs={{0,4},{4,8},{8,12},{12,16},{16,20},{20,24},{24,28},{1,5},{5,9},{9,... | collective-permute-start | bytes 20 | tf_op jit(solution)/shard_map/ppermute | solution.py:14
  11.9 1.3 collective-permute-start.4
  13.1 1.3 collective-permute-start.2
  14.4 1.3 collective-permute-start
  15.7 7.7 %collective-permute-start.10 = (s32[1]{0:T(128)}, s32[1]{0:T(128)}, u32[]{:S(2)}, u32[]{:S(2)}) collective-permute-start(s32[1]{0:T(128)} %bitcast.49), channel_id=1, source_target_pairs={{0,12},{4,16},{8,20},{12,24},{16,28},{1,13},{5,17},{9,21},{13,25},... | collective-permute-start | bytes 20 | tf_op jit(solution)/shard_map/ppermute | solution.py:14
  23.4 1.3 %fusion.23 = (s32[1,1]{1,0:T(1,128)}, s32[1,1]{1,0:T(1,128)}) fusion(s32[1,2]{1,0:T(1,128)} %param.7), kind=kLoop, calls=%fused_computation.45 | loop fusion | bytes 16 | tf_op jit(solution)/shard_map/slice | solution.py:34
  33.7 1.6 %fusion.22 = (s32[1,1]{1,0:T(1,128)}, s32[1,1]{1,0:T(1,128)}, s32[1,1]{1,0:T(1,128)}, s32[1,1]{1,0:T(1,128)}, s32[1,1]{1,0:T(1,128)}, /*index=5*/s32[1,1]{1,0:T(1,128)}, s32[1,1]{1,0:T(1,128)}) fusion(s32[1,7]{1,0:T(1,128)} %param.9), kind=kLoop, calls=%fused_computation.44 | loop fusion | bytes 56 | tf_op jit(solution)/shard_map/slice | solution.py:36
  44.2 1.7 %convert_element_type.10 = bf16[1,128,4096]{2,1,0:T(8,128)(2,1)S(1)} convert(f32[1,128,4096]{2,1,0:T(8,128)} %param.5) | non-fusion elementwise | flops 524288 | bytes 3145728 | tf_op jit(solution)/shard_map/convert_element_type | solution.py:33
  50.4 0.6 fusion.14
  51.0 0.2 bitcast_convert_fusion.6
  51.2 5.9 %collective-permute-start.8 = (s32[1]{0:T(128)}, s32[1]{0:T(128)}, u32[]{:S(2)}, u32[]{:S(2)}) collective-permute-start(s32[1]{0:T(128)} %bitcast.41), channel_id=1, source_target_pairs={{0,8},{4,12},{8,16},{12,20},{16,24},{20,28},{1,9},{5,13},{9,17},{1... | collective-permute-start | bytes 20 | tf_op jit(solution)/shard_map/ppermute | solution.py:14
  57.1 0.7 fusion.18
  57.8 1.3 %collective-permute-start.11 = (bf16[1,128,256]{2,1,0:T(8,128)(2,1)S(1)}, bf16[1,128,256]{2,1,0:T(8,128)(2,1)S(1)}, u32[]{:S(2)}, u32[]{:S(2)}) collective-permute-start(bf16[1,128,256]{2,1,0:T(8,128)(2,1)S(1)} %get-tuple-element.83), channel_id=1, source_target_pairs={{0,12},{4,16},{8,20},{12,24},{16,28},{1,13},{5,17},{9,21},{13,25},... | collective-permute-start | bytes 196616 | tf_op jit(solution)/shard_map/ppermute | solution.py:14
  59.1 0.6 fusion.17
  59.8 2.9 %collective-permute-start.9 = (bf16[1,128,256]{2,1,0:T(8,128)(2,1)S(1)}, bf16[1,128,256]{2,1,0:T(8,128)(2,1)S(1)}, u32[]{:S(2)}, u32[]{:S(2)}) collective-permute-start(bf16[1,128,256]{2,1,0:T(8,128)(2,1)S(1)} %get-tuple-element.84), channel_id=1, source_target_pairs={{0,8},{4,12},{8,16},{12,20},{16,24},{20,28},{1,9},{5,13},{9,17},{1... | collective-permute-start | bytes 196616 | tf_op jit(solution)/shard_map/ppermute | solution.py:14
  62.6 0.6 fusion.16
  63.3 1.3 %collective-permute-start.7 = (bf16[1,128,256]{2,1,0:T(8,128)(2,1)S(1)}, bf16[1,128,256]{2,1,0:T(8,128)(2,1)S(1)}, u32[]{:S(2)}, u32[]{:S(2)}) collective-permute-start(bf16[1,128,256]{2,1,0:T(8,128)(2,1)S(1)} %get-tuple-element.85), channel_id=1, source_target_pairs={{0,4},{4,8},{8,12},{12,16},{16,20},{20,24},{24,28},{1,5},{5,9},{9,... | collective-permute-start | bytes 196616 | tf_op jit(solution)/shard_map/ppermute | solution.py:14
  64.6 0.6 fusion.15
  65.3 1.3 collective-permute-start.5
  66.6 0.6 fusion.20
  67.2 1.3 collective-permute-start.3
  68.5 0.7 fusion.19
  69.2 1.3 collective-permute-start.1
  70.6 4.5 %collective-permute-done.3 = bf16[1,128,256]{2,1,0:T(8,128)(2,1)S(1)} collective-permute-done((bf16[1,128,256]{2,1,0:T(8,128)(2,1)S(1)}, bf16[1,128,256]{2,1,0:T(8,128)(2,1)S(1)}, u32[]{:S(2)}, u32[]{:S(2)}) %collective-permute-start.3) | collective-permute-done | bytes 65568 | tf_op jit(solution)/shard_map/ppermute | solution.py:14
  75.1 1.9 %collective-permute-done.1 = bf16[1,128,256]{2,1,0:T(8,128)(2,1)S(1)} collective-permute-done((bf16[1,128,256]{2,1,0:T(8,128)(2,1)S(1)}, bf16[1,128,256]{2,1,0:T(8,128)(2,1)S(1)}, u32[]{:S(2)}, u32[]{:S(2)}) %collective-permute-start.1) | collective-permute-done | bytes 65568 | tf_op jit(solution)/shard_map/ppermute | solution.py:14
  77.0 15.4 %all-gather.2.cloned.1.call-done = bf16[4,256,2048]{2,1,0:T(8,128)(2,1)} async-done(((bf16[4,256,512]{2,1,0:T(8,128)(2,1)}), bf16[4,256,2048]{2,1,0:T(8,128)(2,1)}) %all-gather.2.cloned.1.call-update) | async-done | bytes 4194320 | tf_op jit(solution)/shard_map/all_gather | solution.py:52
  92.4 4.1 %convolution_bitcast_fusion = f32[128,2048]{1,0:T(8,128)} fusion(bf16[4,256,2048]{2,1,0:T(8,128)(2,1)} %all-gather.2.cloned.1.call-done, f32[128,256]{1,0:T(8,128)S(1)} %bitcast_convert_fusion, f32[4]{0:T(128)S(1)} %fusion.20, f32[128,256]{1,0:T(8,128)S(1)} %bitcast_convert_fusion.1, f32[4]{0:T(128)S(1)} %fusion.19, f32[128,256]{1,0:T(8,128)S(1)} %bitcast_convert_fusion.2, ...), kind=kOutput, calls=%fused_computation | convolution fusion | flops 538705920 | bytes 6160496 | tf_op jit(solution)/shard_map/tfk,tkv->fv/dot_general | solution.py:49
  96.5 0.0 reduce-scatter.2.cloned.1.call-update
  96.5 25.9 %reduce-scatter.2.cloned.1.call-done = f32[128,512]{1,0:T(8,128)} async-done(((f32[128,2048]{1,0:T(8,128)}), f32[128,512]{1,0:T(8,128)}) %reduce-scatter.2.cloned.1.call-update) | async-done | bytes 262160 | tf_op jit(solution)/shard_map/reduce_scatter | solution.py:55
  (17 shorter events, 0.1 us)
Async XLA Ops:
  6.5 85.9 %all-gather.2.cloned.1.call-start = ((), (), s32[]{:S(2)}) async-start(), calls=%async_computation.1 | async-start | bytes 5242880 | tf_op jit(solution)/shard_map/all_gather | solution.py:52
  7.3 115.2 %reduce-scatter.2.cloned.1.call-start = ((), (), s32[]{:S(2)}) async-start(), calls=%async_computation.2 | async-start | bytes 1310720 | tf_op jit(solution)/shard_map/reduce_scatter | solution.py:55
  8.9 42.3 %collective-permute-start.6 = (s32[1]{0:T(128)}, s32[1]{0:T(128)}, u32[]{:S(2)}, u32[]{:S(2)}) collective-permute-start(s32[1]{0:T(128)} %bitcast.33), channel_id=1, source_target_pairs={{0,4},{4,8},{8,12},{12,16},{16,20},{20,24},{24,28},{1,5},{5,9},{9,... | collective-permute-start | bytes 20 | tf_op jit(solution)/shard_map/ppermute | solution.py:14
  11.9 46.0 %collective-permute-start.4 = (s32[1]{0:T(128)}, s32[1]{0:T(128)}, u32[]{:S(2)}, u32[]{:S(2)}) collective-permute-start(s32[1]{0:T(128)} %bitcast.25), channel_id=1, source_target_pairs={{4,0},{8,4},{12,8},{16,12},{20,16},{24,20},{28,24},{5,1},{9,5},{13... | collective-permute-start | bytes 20 | tf_op jit(solution)/shard_map/ppermute | solution.py:14
  13.1 46.6 %collective-permute-start.2 = (s32[1]{0:T(128)}, s32[1]{0:T(128)}, u32[]{:S(2)}, u32[]{:S(2)}) collective-permute-start(s32[1]{0:T(128)} %bitcast.17), channel_id=1, source_target_pairs={{8,0},{12,4},{16,8},{20,12},{24,16},{28,20},{9,1},{13,5},{17,9},{2... | collective-permute-start | bytes 20 | tf_op jit(solution)/shard_map/ppermute | solution.py:14
  14.4 48.8 %collective-permute-start = (s32[1]{0:T(128)}, s32[1]{0:T(128)}, u32[]{:S(2)}, u32[]{:S(2)}) collective-permute-start(s32[1]{0:T(128)} %bitcast.9), channel_id=1, source_target_pairs={{12,0},{16,4},{20,8},{24,12},{28,16},{13,1},{17,5},{21,9},{25,13},... | collective-permute-start | bytes 20 | tf_op jit(solution)/shard_map/ppermute | solution.py:14
  15.7 49.5 %collective-permute-start.10 = (s32[1]{0:T(128)}, s32[1]{0:T(128)}, u32[]{:S(2)}, u32[]{:S(2)}) collective-permute-start(s32[1]{0:T(128)} %bitcast.49), channel_id=1, source_target_pairs={{0,12},{4,16},{8,20},{12,24},{16,28},{1,13},{5,17},{9,21},{13,25},... | collective-permute-start | bytes 20 | tf_op jit(solution)/shard_map/ppermute | solution.py:14
  51.2 16.0 %collective-permute-start.8 = (s32[1]{0:T(128)}, s32[1]{0:T(128)}, u32[]{:S(2)}, u32[]{:S(2)}) collective-permute-start(s32[1]{0:T(128)} %bitcast.41), channel_id=1, source_target_pairs={{0,8},{4,12},{8,16},{12,20},{16,24},{20,28},{1,9},{5,13},{9,17},{1... | collective-permute-start | bytes 20 | tf_op jit(solution)/shard_map/ppermute | solution.py:14
  57.8 11.4 %collective-permute-start.11 = (bf16[1,128,256]{2,1,0:T(8,128)(2,1)S(1)}, bf16[1,128,256]{2,1,0:T(8,128)(2,1)S(1)}, u32[]{:S(2)}, u32[]{:S(2)}) collective-permute-start(bf16[1,128,256]{2,1,0:T(8,128)(2,1)S(1)} %get-tuple-element.83), channel_id=1, source_target_pairs={{0,12},{4,16},{8,20},{12,24},{16,28},{1,13},{5,17},{9,21},{13,25},... | collective-permute-start | bytes 196616 | tf_op jit(solution)/shard_map/ppermute | solution.py:14
  59.8 10.7 %collective-permute-start.9 = (bf16[1,128,256]{2,1,0:T(8,128)(2,1)S(1)}, bf16[1,128,256]{2,1,0:T(8,128)(2,1)S(1)}, u32[]{:S(2)}, u32[]{:S(2)}) collective-permute-start(bf16[1,128,256]{2,1,0:T(8,128)(2,1)S(1)} %get-tuple-element.84), channel_id=1, source_target_pairs={{0,8},{4,12},{8,16},{12,20},{16,24},{20,28},{1,9},{5,13},{9,17},{1... | collective-permute-start | bytes 196616 | tf_op jit(solution)/shard_map/ppermute | solution.py:14
  63.3 7.2 %collective-permute-start.7 = (bf16[1,128,256]{2,1,0:T(8,128)(2,1)S(1)}, bf16[1,128,256]{2,1,0:T(8,128)(2,1)S(1)}, u32[]{:S(2)}, u32[]{:S(2)}) collective-permute-start(bf16[1,128,256]{2,1,0:T(8,128)(2,1)S(1)} %get-tuple-element.85), channel_id=1, source_target_pairs={{0,4},{4,8},{8,12},{12,16},{16,20},{20,24},{24,28},{1,5},{5,9},{9,... | collective-permute-start | bytes 196616 | tf_op jit(solution)/shard_map/ppermute | solution.py:14
  65.3 5.3 %collective-permute-start.5 = (bf16[1,128,256]{2,1,0:T(8,128)(2,1)S(1)}, bf16[1,128,256]{2,1,0:T(8,128)(2,1)S(1)}, u32[]{:S(2)}, u32[]{:S(2)}) collective-permute-start(bf16[1,128,256]{2,1,0:T(8,128)(2,1)S(1)} %get-tuple-element.86), channel_id=1, source_target_pairs={{4,0},{8,4},{12,8},{16,12},{20,16},{24,20},{28,24},{5,1},{9,5},{13... | collective-permute-start | bytes 196616 | tf_op jit(solution)/shard_map/ppermute | solution.py:14
  67.2 7.9 %collective-permute-start.3 = (bf16[1,128,256]{2,1,0:T(8,128)(2,1)S(1)}, bf16[1,128,256]{2,1,0:T(8,128)(2,1)S(1)}, u32[]{:S(2)}, u32[]{:S(2)}) collective-permute-start(bf16[1,128,256]{2,1,0:T(8,128)(2,1)S(1)} %get-tuple-element.87), channel_id=1, source_target_pairs={{8,0},{12,4},{16,8},{20,12},{24,16},{28,20},{9,1},{13,5},{17,9},{2... | collective-permute-start | bytes 196616 | tf_op jit(solution)/shard_map/ppermute | solution.py:14
  69.2 7.8 %collective-permute-start.1 = (bf16[1,128,256]{2,1,0:T(8,128)(2,1)S(1)}, bf16[1,128,256]{2,1,0:T(8,128)(2,1)S(1)}, u32[]{:S(2)}, u32[]{:S(2)}) collective-permute-start(bf16[1,128,256]{2,1,0:T(8,128)(2,1)S(1)} %get-tuple-element.88), channel_id=1, source_target_pairs={{12,0},{16,4},{20,8},{24,12},{28,16},{13,1},{17,5},{21,9},{25,13},... | collective-permute-start | bytes 196616 | tf_op jit(solution)/shard_map/ppermute | solution.py:14
Sparse Core Ops, SparseCore 0:
  8.9 83.4 all-gather.1
  96.6 25.7 reduce-scatter.1
where the time goes:
time: 130 us; the launch traced here: 129 us
  waiting for transfers between devices  48.5 us (37%)
  between operations  36 us (28%)
  starting transfers between devices  29.8 us (23%)
  other arithmetic  6.48 us (5%)
  local copies, waits for them, and re-layouts  4.5 us (3%)
  matrix products  4.07 us (3%)
    ppermute x12, starting transfers between devices, shifted(): return lax.ppermute(x, axis, pairs)  29.8 us
    reduce_scatter x1, waiting for transfers between devices, body(): lax.psum_scatter(partial_image, 'det', scatter_dimension=1, tiled=True)  25.9 us
    all_gather x1, waiting for transfers between devices, body(): lax.all_gather(tables, 'det', axis=2, tiled=True)  15.4 us
    ppermute x12, waiting for transfers between devices, shifted(): return lax.ppermute(x, axis, pairs)  6.42 us
    another operation x14, other arithmetic  4.75 us
    dot_general x1, matrix products, body(): jnp.einsum('tfk,tkv->fv', binned, lax.all_gather(tables, 'det', axis=2, t...  4.07 us
  transfers between devices with their start and end apart: 14, of which 4 were waited for; matrix products, arithmetic and copies ran while one was open for 8% of the time, Pallas kernels for 0%

commit v1 on v0

--- a/solution.py
+++ b/solution.py
@@ -46,12 +46,21 @@
         everything = jnp.ones(arrived_slots.shape, jnp.bool_)
         stacked = stacked + bin_windows(arrived_windows, arrived_slots, everything)
     binned = stacked.astype(jnp.bfloat16)
-    partial_image = jnp.einsum(
-        "tfk,tkv->fv",
-        binned,
-        lax.all_gather(tables, "det", axis=2, tiled=True),
-        preferred_element_type=jnp.float32,
-    )
+    ways, here, lap = (lax.axis_size("det"), lax.axis_index("det"), tables.shape[2])
+    earlier, later = ([], [])
+    going_up = going_down = tables
+    for far in range(ways // 2 + 1):
+        earlier.append(
+            jnp.einsum("tfk,tkv->fv", binned, going_up, preferred_element_type=jnp.float32)
+        )
+        if 0 < far < ways - ways // 2:
+            later.append(
+                jnp.einsum("tfk,tkv->fv", binned, going_down, preferred_element_type=jnp.float32)
+            )
+        going_up = lax.ppermute(going_up, "det", [(d, (d + 1) % ways) for d in range(ways)])
+        going_down = lax.ppermute(going_down, "det", [(d, (d - 1) % ways) for d in range(ways)])
+    line = jnp.concatenate([*earlier[::-1], *later], axis=1)
+    partial_image = jnp.roll(line, (here - ways // 2) * earlier[0].shape[1], axis=1)
     return lax.psum_scatter(partial_image, "det", scatter_dimension=1, tiled=True)
 
 

time: 130 us -> 151 us (1.16)
  waiting for transfers between devices: 48.5 us -> 65.2 us
  starting transfers between devices: 29.8 us -> 36.2 us
  matrix products: 4.07 us -> 1.24 us
    ppermute x0 -> x3, waiting for transfers between devices: none -> 20.5 us  [the longest x2 20.5 us: body(): lax.ppermute(going_up, 'det', [(d, (d + 1) % ways) for d in range(ways)])]
    all_gather x1 -> x0, waiting for transfers between devices: 15.4 us -> none  [body(): lax.all_gather(tables, 'det', axis=2, tiled=True)]
    ppermute x12, waiting for transfers between devices: 6.42 us -> 14.3 us  [shifted(): return lax.ppermute(x, axis, pairs)]
    ppermute x0 -> x3, starting transfers between devices: none -> 5.14 us  [the longest x2 3.11 us: body(): lax.ppermute(going_up, 'det', [(d, (d + 1) % ways) for d in range(ways)])]
    reduce_scatter x1, waiting for transfers between devices: 25.9 us -> 30.4 us  [body(): lax.psum_scatter(partial_image, 'det', scatter_dimension=1, tiled=True)]
    dot_general x1 -> x4, matrix products: 4.07 us -> 1.24 us  [the longest x3 0.93 us: body(): jnp.einsum('tfk,tkv->fv', binned, going_up, preferred_element_type=jnp.fl...]
  transfers between devices with their start and end apart: 14 -> 16, of which waited for: 4 -> 9; matrix products, arithmetic and copies ran while one was open for 8% -> 8% of each run, Pallas kernels for 0% -> 0%
where the time goes in v1:
time: 151 us; the launch traced here: 150 us
  waiting for transfers between devices  65.2 us (43%)
  starting transfers between devices  36.2 us (24%)
  between operations  36.1 us (24%)
  other arithmetic  6.75 us (4%)
  local copies, waits for them, and re-layouts  4.79 us (3%)
    ppermute x12, starting transfers between devices, shifted(): return lax.ppermute(x, axis, pairs)  31 us
    reduce_scatter x1, waiting for transfers between devices, body(): lax.psum_scatter(partial_image, 'det', scatter_dimension=1, tiled=True)  30.4 us
    ppermute x2, waiting for transfers between devices, body(): lax.ppermute(going_up, 'det', [(d, (d + 1) % ways) for d in range(ways)])  20.5 us
    ppermute x12, waiting for transfers between devices, shifted(): return lax.ppermute(x, axis, pairs)  14.3 us
    another operation x14, other arithmetic  4.73 us
    ppermute x2, starting transfers between devices, body(): lax.ppermute(going_up, 'det', [(d, (d + 1) % ways) for d in range(ways)])  3.11 us
  transfers between devices with their start and end apart: 16, of which 9 were waited for; matrix products, arithmetic and copies ran while one was open for 8% of the time, Pallas kernels for 0%

profile of v1, /device:TPU:0, one launch (start us, length us, event | category | flops | bytes accessed | tf_op | source)
XLA Modules:
  0.0 150.2 jit_solution(13815892210423949015)
XLA Ops:
  6.5 3.1 %collective-permute-start.12 = (bf16[4,256,512]{2,1,0:T(8,128)(2,1)}, bf16[4,256,512]{2,1,0:T(8,128)(2,1)S(1)}, u32[]{:S(2)}, u32[]{:S(2)}) collective-permute-start(bf16[4,256,512]{2,1,0:T(8,128)(2,1)} %param.6), channel_id=1, source_target_pairs={{0,1},{1,2},{2,3},{3,0},{4,5},{5,6},{6,7},{7,4},{8,9},{9,10},{10,1... | collective-permute-start | bytes 3145736 | tf_op jit(solution)/shard_map/ppermute | solution.py:60
  9.6 2.0 %collective-permute-start.14 = (bf16[4,256,512]{2,1,0:T(8,128)(2,1)}, bf16[4,256,512]{2,1,0:T(8,128)(2,1)S(1)}, u32[]{:S(2)}, u32[]{:S(2)}) collective-permute-start(bf16[4,256,512]{2,1,0:T(8,128)(2,1)} %param.6), channel_id=1, source_target_pairs={{0,3},{1,0},{2,1},{3,2},{4,7},{5,4},{6,5},{7,6},{8,11},{9,8},{10,9... | collective-permute-start | bytes 3145736 | tf_op jit(solution)/shard_map/ppermute | solution.py:61
  11.6 1.3 fusion.9
  20.4 1.6 %fusion.8 = (s32[1,1]{1,0:T(1,128)}, s32[1,1]{1,0:T(1,128)}, s32[1,1]{1,0:T(1,128)}, s32[1,1]{1,0:T(1,128)}, s32[1,1]{1,0:T(1,128)}, /*index=5*/s32[1,1]{1,0:T(1,128)}, s32[1,1]{1,0:T(1,128)}) fusion(s32[1,7]{1,0:T(1,128)} %param.9), kind=kLoop, calls=%fused_computation.42 | loop fusion | bytes 56 | tf_op jit(solution)/shard_map/slice | solution.py:36
  31.1 1.7 %convert_element_type.10 = bf16[1,128,4096]{2,1,0:T(8,128)(2,1)S(1)} convert(f32[1,128,4096]{2,1,0:T(8,128)} %param.5) | non-fusion elementwise | flops 524288 | bytes 3145728 | tf_op jit(solution)/shard_map/convert_element_type | solution.py:33
  37.5 2.6 %collective-permute-start.11 = (bf16[1,128,256]{2,1,0:T(8,128)(2,1)S(1)}, bf16[1,128,256]{2,1,0:T(8,128)(2,1)S(1)}, u32[]{:S(2)}, u32[]{:S(2)}) collective-permute-start(bf16[1,128,256]{2,1,0:T(8,128)(2,1)S(1)} %get-tuple-element.83), channel_id=1, source_target_pairs={{0,12},{4,16},{8,20},{12,24},{16,28},{1,13},{5,17},{9,21},{13,25},... | collective-permute-start | bytes 196616 | tf_op jit(solution)/shard_map/ppermute | solution.py:14
  40.1 3.4 %collective-permute-start.9 = (bf16[1,128,256]{2,1,0:T(8,128)(2,1)S(1)}, bf16[1,128,256]{2,1,0:T(8,128)(2,1)S(1)}, u32[]{:S(2)}, u32[]{:S(2)}) collective-permute-start(bf16[1,128,256]{2,1,0:T(8,128)(2,1)S(1)} %get-tuple-element.84), channel_id=1, source_target_pairs={{0,8},{4,12},{8,16},{12,20},{16,24},{20,28},{1,9},{5,13},{9,17},{1... | collective-permute-start | bytes 196616 | tf_op jit(solution)/shard_map/ppermute | solution.py:14
  43.5 0.7 fusion.7
  44.2 1.3 collective-permute-start
  46.8 0.7 fusion
  47.4 1.8 %collective-permute-done = s32[1]{0:T(128)} collective-permute-done((s32[1]{0:T(128)}, s32[1]{0:T(128)}, u32[]{:S(2)}, u32[]{:S(2)}) %collective-permute-start) | collective-permute-done | bytes 36 | tf_op jit(solution)/shard_map/ppermute | solution.py:14
  49.3 1.3 collective-permute-start.2
  50.5 0.6 fusion.1
  51.2 4.1 %collective-permute-done.2 = s32[1]{0:T(128)} collective-permute-done((s32[1]{0:T(128)}, s32[1]{0:T(128)}, u32[]{:S(2)}, u32[]{:S(2)}) %collective-permute-start.2) | collective-permute-done | bytes 36 | tf_op jit(solution)/shard_map/ppermute | solution.py:14
  55.2 1.3 collective-permute-start.4
  56.5 0.6 fusion.2
  57.2 1.1 collective-permute-done.4
  58.3 5.7 %collective-permute-start.6 = (s32[1]{0:T(128)}, s32[1]{0:T(128)}, u32[]{:S(2)}, u32[]{:S(2)}) collective-permute-start(s32[1]{0:T(128)} %bitcast.33), channel_id=1, source_target_pairs={{0,4},{4,8},{8,12},{12,16},{16,20},{20,24},{24,28},{1,5},{5,9},{9,... | collective-permute-start | bytes 20 | tf_op jit(solution)/shard_map/ppermute | solution.py:14
  64.0 0.7 fusion.3
  64.7 4.5 %collective-permute-start.8 = (s32[1]{0:T(128)}, s32[1]{0:T(128)}, u32[]{:S(2)}, u32[]{:S(2)}) collective-permute-start(s32[1]{0:T(128)} %bitcast.41), channel_id=1, source_target_pairs={{0,8},{4,12},{8,16},{12,20},{16,24},{20,28},{1,9},{5,13},{9,17},{1... | collective-permute-start | bytes 20 | tf_op jit(solution)/shard_map/ppermute | solution.py:14
  70.1 1.8 %collective-permute-start.10 = (s32[1]{0:T(128)}, s32[1]{0:T(128)}, u32[]{:S(2)}, u32[]{:S(2)}) collective-permute-start(s32[1]{0:T(128)} %bitcast.49), channel_id=1, source_target_pairs={{0,12},{4,16},{8,20},{12,24},{16,28},{1,13},{5,17},{9,21},{13,25},... | collective-permute-start | bytes 20 | tf_op jit(solution)/shard_map/ppermute | solution.py:14
  71.9 0.7 fusion.5
  72.7 5.5 %collective-permute-start.7 = (bf16[1,128,256]{2,1,0:T(8,128)(2,1)S(1)}, bf16[1,128,256]{2,1,0:T(8,128)(2,1)S(1)}, u32[]{:S(2)}, u32[]{:S(2)}) collective-permute-start(bf16[1,128,256]{2,1,0:T(8,128)(2,1)S(1)} %get-tuple-element.85), channel_id=1, source_target_pairs={{0,4},{4,8},{8,12},{12,16},{16,20},{20,24},{24,28},{1,5},{5,9},{9,... | collective-permute-start | bytes 196616 | tf_op jit(solution)/shard_map/ppermute | solution.py:14
  78.2 0.6 fusion.6
  78.7 1.3 collective-permute-start.5
  80.1 1.3 collective-permute-start.3
  81.4 1.3 collective-permute-start.1
  82.8 3.6 %collective-permute-done.3 = bf16[1,128,256]{2,1,0:T(8,128)(2,1)S(1)} collective-permute-done((bf16[1,128,256]{2,1,0:T(8,128)(2,1)S(1)}, bf16[1,128,256]{2,1,0:T(8,128)(2,1)S(1)}, u32[]{:S(2)}, u32[]{:S(2)}) %collective-permute-start.3) | collective-permute-done | bytes 65568 | tf_op jit(solution)/shard_map/ppermute | solution.py:14
  86.5 3.2 %collective-permute-done.1 = bf16[1,128,256]{2,1,0:T(8,128)(2,1)S(1)} collective-permute-done((bf16[1,128,256]{2,1,0:T(8,128)(2,1)S(1)}, bf16[1,128,256]{2,1,0:T(8,128)(2,1)S(1)}, u32[]{:S(2)}, u32[]{:S(2)}) %collective-permute-start.1) | collective-permute-done | bytes 65568 | tf_op jit(solution)/shard_map/ppermute | solution.py:14
  90.0 20.5 %collective-permute-done.13 = bf16[4,256,512]{2,1,0:T(8,128)(2,1)S(1)} collective-permute-done((bf16[4,256,512]{2,1,0:T(8,128)(2,1)S(1)}, bf16[4,256,512]{2,1,0:T(8,128)(2,1)S(1)}, u32[]{:S(2)}, u32[]{:S(2)}) %collective-permute-start.13) | collective-permute-done | bytes 1048608 | tf_op jit(solution)/shard_map/ppermute | solution.py:60
  111.8 1.1 constant_dynamic-slice_fusion
  113.0 30.4 %reduce-scatter.2.cloned.1.call-done = f32[128,512]{1,0:T(8,128)} async-done(((f32[128,2048]{1,0:T(8,128)}), f32[128,512]{1,0:T(8,128)}) %reduce-scatter.2.cloned.1.call-update) | async-done | bytes 262160 | tf_op jit(solution)/shard_map/reduce_scatter | solution.py:64
  (33 shorter events, 3.1 us)
Async XLA Ops:
  6.5 136.8 %reduce-scatter.2.cloned.1.call-start = ((), (), s32[]{:S(2)}) async-start(), calls=%async_computation.1 | async-start | bytes 1310720 | tf_op jit(solution)/shard_map/reduce_scatter | solution.py:64
  6.5 76.2 %collective-permute-start.12 = (bf16[4,256,512]{2,1,0:T(8,128)(2,1)}, bf16[4,256,512]{2,1,0:T(8,128)(2,1)S(1)}, u32[]{:S(2)}, u32[]{:S(2)}) collective-permute-start(bf16[4,256,512]{2,1,0:T(8,128)(2,1)} %param.6), channel_id=1, source_target_pairs={{0,1},{1,2},{2,3},{3,0},{4,5},{5,6},{6,7},{7,4},{8,9},{9,10},{10,1... | collective-permute-start | bytes 3145736 | tf_op jit(solution)/shard_map/ppermute | solution.py:60
  9.6 101.8 %collective-permute-start.14 = (bf16[4,256,512]{2,1,0:T(8,128)(2,1)}, bf16[4,256,512]{2,1,0:T(8,128)(2,1)S(1)}, u32[]{:S(2)}, u32[]{:S(2)}) collective-permute-start(bf16[4,256,512]{2,1,0:T(8,128)(2,1)} %param.6), channel_id=1, source_target_pairs={{0,3},{1,0},{2,1},{3,2},{4,7},{5,4},{6,5},{7,6},{8,11},{9,8},{10,9... | collective-permute-start | bytes 3145736 | tf_op jit(solution)/shard_map/ppermute | solution.py:61
  31.0 12.5 %copy-start.1 = (s32[1,7]{1,0:T(1,128)S(1)}, s32[1,7]{1,0:T(1,128)}, u32[]{:S(2)}) copy-start(s32[1,7]{1,0:T(1,128)} %param.8) | copy-start | bytes 88
  37.5 41.2 %collective-permute-start.11 = (bf16[1,128,256]{2,1,0:T(8,128)(2,1)S(1)}, bf16[1,128,256]{2,1,0:T(8,128)(2,1)S(1)}, u32[]{:S(2)}, u32[]{:S(2)}) collective-permute-start(bf16[1,128,256]{2,1,0:T(8,128)(2,1)S(1)} %get-tuple-element.83), channel_id=1, source_target_pairs={{0,12},{4,16},{8,20},{12,24},{16,28},{1,13},{5,17},{9,21},{13,25},... | collective-permute-start | bytes 196616 | tf_op jit(solution)/shard_map/ppermute | solution.py:14
  40.1 40.0 %collective-permute-start.9 = (bf16[1,128,256]{2,1,0:T(8,128)(2,1)S(1)}, bf16[1,128,256]{2,1,0:T(8,128)(2,1)S(1)}, u32[]{:S(2)}, u32[]{:S(2)}) collective-permute-start(bf16[1,128,256]{2,1,0:T(8,128)(2,1)S(1)} %get-tuple-element.84), channel_id=1, source_target_pairs={{0,8},{4,12},{8,16},{12,20},{16,24},{20,28},{1,9},{5,13},{9,17},{1... | collective-permute-start | bytes 196616 | tf_op jit(solution)/shard_map/ppermute | solution.py:14
  44.2 5.0 %collective-permute-start = (s32[1]{0:T(128)}, s32[1]{0:T(128)}, u32[]{:S(2)}, u32[]{:S(2)}) collective-permute-start(s32[1]{0:T(128)} %bitcast.9), channel_id=1, source_target_pairs={{12,0},{16,4},{20,8},{24,12},{28,16},{13,1},{17,5},{21,9},{25,13},... | collective-permute-start | bytes 20 | tf_op jit(solution)/shard_map/ppermute | solution.py:14
  49.3 6.0 %collective-permute-start.2 = (s32[1]{0:T(128)}, s32[1]{0:T(128)}, u32[]{:S(2)}, u32[]{:S(2)}) collective-permute-start(s32[1]{0:T(128)} %bitcast.17), channel_id=1, source_target_pairs={{8,0},{12,4},{16,8},{20,12},{24,16},{28,20},{9,1},{13,5},{17,9},{2... | collective-permute-start | bytes 20 | tf_op jit(solution)/shard_map/ppermute | solution.py:14
  55.2 3.1 %collective-permute-start.4 = (s32[1]{0:T(128)}, s32[1]{0:T(128)}, u32[]{:S(2)}, u32[]{:S(2)}) collective-permute-start(s32[1]{0:T(128)} %bitcast.25), channel_id=1, source_target_pairs={{4,0},{8,4},{12,8},{16,12},{20,16},{24,20},{28,24},{5,1},{9,5},{13... | collective-permute-start | bytes 20 | tf_op jit(solution)/shard_map/ppermute | solution.py:14
  58.3 6.4 %collective-permute-start.6 = (s32[1]{0:T(128)}, s32[1]{0:T(128)}, u32[]{:S(2)}, u32[]{:S(2)}) collective-permute-start(s32[1]{0:T(128)} %bitcast.33), channel_id=1, source_target_pairs={{0,4},{4,8},{8,12},{12,16},{16,20},{20,24},{24,28},{1,5},{5,9},{9,... | collective-permute-start | bytes 20 | tf_op jit(solution)/shard_map/ppermute | solution.py:14
  64.7 5.4 %collective-permute-start.8 = (s32[1]{0:T(128)}, s32[1]{0:T(128)}, u32[]{:S(2)}, u32[]{:S(2)}) collective-permute-start(s32[1]{0:T(128)} %bitcast.41), channel_id=1, source_target_pairs={{0,8},{4,12},{8,16},{12,20},{16,24},{20,28},{1,9},{5,13},{9,17},{1... | collective-permute-start | bytes 20 | tf_op jit(solution)/shard_map/ppermute | solution.py:14
  70.1 2.6 %collective-permute-start.10 = (s32[1]{0:T(128)}, s32[1]{0:T(128)}, u32[]{:S(2)}, u32[]{:S(2)}) collective-permute-start(s32[1]{0:T(128)} %bitcast.49), channel_id=1, source_target_pairs={{0,12},{4,16},{8,20},{12,24},{16,28},{1,13},{5,17},{9,21},{13,25},... | collective-permute-start | bytes 20 | tf_op jit(solution)/shard_map/ppermute | solution.py:14
  72.7 8.7 %collective-permute-start.7 = (bf16[1,128,256]{2,1,0:T(8,128)(2,1)S(1)}, bf16[1,128,256]{2,1,0:T(8,128)(2,1)S(1)}, u32[]{:S(2)}, u32[]{:S(2)}) collective-permute-start(bf16[1,128,256]{2,1,0:T(8,128)(2,1)S(1)} %get-tuple-element.85), channel_id=1, source_target_pairs={{0,4},{4,8},{8,12},{12,16},{16,20},{20,24},{24,28},{1,5},{5,9},{9,... | collective-permute-start | bytes 196616 | tf_op jit(solution)/shard_map/ppermute | solution.py:14
  78.7 4.1 %collective-permute-start.5 = (bf16[1,128,256]{2,1,0:T(8,128)(2,1)S(1)}, bf16[1,128,256]{2,1,0:T(8,128)(2,1)S(1)}, u32[]{:S(2)}, u32[]{:S(2)}) collective-permute-start(bf16[1,128,256]{2,1,0:T(8,128)(2,1)S(1)} %get-tuple-element.86), channel_id=1, source_target_pairs={{4,0},{8,4},{12,8},{16,12},{20,16},{24,20},{28,24},{5,1},{9,5},{13... | collective-permute-start | bytes 196616 | tf_op jit(solution)/shard_map/ppermute | solution.py:14
  80.1 6.4 %collective-permute-start.3 = (bf16[1,128,256]{2,1,0:T(8,128)(2,1)S(1)}, bf16[1,128,256]{2,1,0:T(8,128)(2,1)S(1)}, u32[]{:S(2)}, u32[]{:S(2)}) collective-permute-start(bf16[1,128,256]{2,1,0:T(8,128)(2,1)S(1)} %get-tuple-element.87), channel_id=1, source_target_pairs={{8,0},{12,4},{16,8},{20,12},{24,16},{28,20},{9,1},{13,5},{17,9},{2... | collective-permute-start | bytes 196616 | tf_op jit(solution)/shard_map/ppermute | solution.py:14
  81.4 8.2 %collective-permute-start.1 = (bf16[1,128,256]{2,1,0:T(8,128)(2,1)S(1)}, bf16[1,128,256]{2,1,0:T(8,128)(2,1)S(1)}, u32[]{:S(2)}, u32[]{:S(2)}) collective-permute-start(bf16[1,128,256]{2,1,0:T(8,128)(2,1)S(1)} %get-tuple-element.88), channel_id=1, source_target_pairs={{12,0},{16,4},{20,8},{24,12},{28,16},{13,1},{17,5},{21,9},{25,13},... | collective-permute-start | bytes 196616 | tf_op jit(solution)/shard_map/ppermute | solution.py:14
  82.7 27.7 %collective-permute-start.13 = (bf16[4,256,512]{2,1,0:T(8,128)(2,1)S(1)}, bf16[4,256,512]{2,1,0:T(8,128)(2,1)S(1)}, u32[]{:S(2)}, u32[]{:S(2)}) collective-permute-start(bf16[4,256,512]{2,1,0:T(8,128)(2,1)S(1)} %collective-permute-done.12), channel_id=1, source_target_pairs={{0,1},{1,2},{2,3},{3,0},{4,5},{5,6},{6,7},{7,4},{8,9},{9,10},{10,1... | collective-permute-start | bytes 3145736 | tf_op jit(solution)/shard_map/ppermute | solution.py:60
  90.0 21.1 %copy-start = (bf16[4,256,512]{2,1,0:T(8,128)(2,1)S(1)}, bf16[4,256,512]{2,1,0:T(8,128)(2,1)}, u32[]{:S(2)}) copy-start(bf16[4,256,512]{2,1,0:T(8,128)(2,1)} %param.6) | copy-start | bytes 3145732
Sparse Core Ops, SparseCore 0:
  113.1 30.2 reduce-scatter.1
